TPU v7x, 32 devices: a whole 2x2x4 slice. The times are simulated.
32 devices in a mesh: dp: 4 (over z), tp: 8 (over y, x, core).
Axes of the slice: x: 2, y: 2, z: 4, core: 2. Of those that a mesh axis runs over, the one named last changes fastest.
Arguments:
- hidden: bfloat16 [8192, 576], P('dp')
- w_final: float32 [576], replicated
- emb_table: bfloat16 [49152, 576], P('tp')
- teacher: bfloat16 [8192, 49152], P('dp', 'tp')
- tok_mask: float32 [8192], P('dp')
Outputs:
- output 1: float32 [], replicated
- output 2: bfloat16 [8192, 576], P('dp')
- output 3: float32 [576], replicated
- output 4: float32 [49152, 576], P('tp')
All inputs are finite; a program needn't handle non-finite values.
Results may differ from a plain program's by a relative error of at most 0.00101509.
Values sent between devices are 32-bit elements.
A program may use at most 1 GiB of HBM per device.

v0:
```python
import jax
import jax.numpy as jnp
from jax import lax
from jax.sharding import PartitionSpec as P

SOFT_CAP = 30.0
NORM_EPS = 1e-6


def final_norm(hid_rows, w_final):
    hid_f = hid_rows.astype(jnp.float32)
    inv_rms = lax.rsqrt(jnp.mean(hid_f * hid_f, axis=-1, keepdims=True) + NORM_EPS)
    normed = hid_f * inv_rms
    return inv_rms, normed, (normed * (1.0 + w_final)).astype(jnp.bfloat16)


def solution(mesh):
    def local_step(hid_rows, w_final, tab_rows, tea_rows, mask_rows):
        mask_sum = lax.psum(jnp.sum(mask_rows), 'dp')
        inv_rms, normed, x_rows = final_norm(hid_rows, w_final)
        logits = lax.dot_general(x_rows, tab_rows, (((1,), (1,)), ((), ())), preferred_element_type=jnp.float32)
        stu_cap = SOFT_CAP * jnp.tanh(logits / SOFT_CAP)
        tea_cap = SOFT_CAP * jnp.tanh(tea_rows.astype(jnp.float32) / SOFT_CAP)
        stu_exp = jnp.exp(stu_cap - SOFT_CAP)
        tea_exp = jnp.exp(tea_cap - SOFT_CAP)
        part_stats = jnp.stack([jnp.sum(stu_exp, axis=-1), jnp.sum(tea_exp, axis=-1), jnp.sum(tea_exp * (tea_cap - stu_cap), axis=-1)], axis=-1)
        tok_stats = lax.psum(part_stats, 'tp')
        stu_sum = tok_stats[:, 0:1]
        tea_sum = tok_stats[:, 1:2]
        kl_rows = tok_stats[:, 2] / tok_stats[:, 1] + jnp.log(tok_stats[:, 0]) - jnp.log(tok_stats[:, 1])
        loss_val = lax.psum(jnp.sum(mask_rows * kl_rows), 'dp') / mask_sum
        weight = (mask_rows / mask_sum)[:, None]
        cap_ratio = stu_cap / SOFT_CAP
        grad_z = ((stu_exp / stu_sum - tea_exp / tea_sum) * weight * (1.0 - cap_ratio * cap_ratio)).astype(jnp.bfloat16)
        grad_x = lax.psum(jnp.dot(grad_z, tab_rows, preferred_element_type=jnp.float32), 'tp')
        grad_table = lax.psum(lax.dot_general(grad_z, x_rows, (((0,), (0,)), ((), ())), preferred_element_type=jnp.float32), 'dp')
        grad_n = grad_x * (1.0 + w_final)
        grad_h = inv_rms * (grad_n - normed * jnp.mean(grad_n * normed, axis=-1, keepdims=True))
        grad_gain = lax.psum(jnp.sum(grad_x * normed, axis=0), 'dp')
        return loss_val, grad_h.astype(jnp.bfloat16), grad_gain, grad_table

    return jax.shard_map(local_step, mesh=mesh, in_specs=(P('dp', None), P(None), P('tp', None), P('dp', 'tp'), P('dp')), out_specs=(P(), P('dp', None), P(None), P('tp', None)), check_vma=False)
```

profile of v0, /device:TPU:0, one launch (start us, length us, event | category | flops | bytes accessed | tf_op | source)
XLA Modules:
  0.0 748.7 jit_solution(6117430896983118505)
XLA Ops:
  7.2 0.0 all-reduce.4.cloned.1.call-start
  7.2 0.7 broadcast_add_fusion
  7.9 2.2 fusion.12
  10.1 0.0 copy-start.1
  10.1 56.1 %fusion.1 = (f32[2048]{0:T(1024)S(1)}, f32[2048]{0:T(1024)S(1)}, f32[2048]{0:T(1024)S(1)}, f32[2048,6144]{1,0:T(8,128)}) fusion(bf16[2048,6144]{1,0:T(8,128)(2,1)} %param.8, bf16[6144,576]{0,1:T(8,128)(2,1)} %param.7, bf16[2048,576]{0,1:T(8,128)(2,1)} %param.5, f32[576]{0:T(1024)S(1)} %broadcast_add_fusion, f32[2048]{0:T(1024)S(1)} %add_rsqrt_fusion), kind=kOutput, calls=%fused_computation.7 | convolution fusion | flops 14651222016 | bytes 84969728 | tf_op jit(solution)/shard_map/dot_general | solution.py:21
  66.2 25.6 %psum.42 = f32[2048,3]{0,1:T(4,128)S(1)} all-reduce(f32[2048,3]{0,1:T(4,128)S(1)} %pad_maximum_fusion), channel_id=1, replica_groups=mesh['dp'=4,'tp'=8] {'tp'}, use_global_device_ids=true, to_apply=%region_4.0 | all-reduce | flops 6144 | bytes 49152 | tf_op jit(solution)/shard_map/psum | solution.py:27
  91.8 0.0 copy-done.1
  91.8 0.6 fusion.17
  92.4 12.8 %psum.44 = f32[]{:T(128)} all-reduce(f32[]{:T(128)} %get-tuple-element.9), channel_id=1, replica_groups=mesh['dp'=4,'tp'=8] {'dp'}, use_global_device_ids=true, to_apply=%region_8.0 | all-reduce | flops 1 | bytes 8 | tf_op jit(solution)/shard_map/psum | solution.py:19
  105.2 0.6 broadcast_divide_fusion
  105.8 0.0 copy-start.2
  105.8 42.1 %multiply_convert_fusion = bf16[2048,6144]{1,0:T(8,128)(2,1)} fusion(bf16[2048,6144]{1,0:T(8,128)(2,1)} %param.8, f32[2048,6144]{1,0:T(8,128)} %get-tuple-element.16, f32[2048]{0:T(1024)S(1)} %broadcast_divide_fusion, f32[2048]{0:T(1024)S(1)} %bitcast.14, f32[2048]{0:T(1024)S(1)} %bitcast.12), kind=kLoop, calls=%fused_computation | loop fusion | flops 188743680 | bytes 100687872 | tf_op jit(solution)/shard_map/convert_element_type | solution.py:34
  148.0 0.0 copy-done.2
  148.0 0.0 copy-start
  148.0 19.4 %fusion.19 = f32[2048,576]{0,1:T(8,128)} fusion(bf16[2048,6144]{1,0:T(8,128)(2,1)} %multiply_convert_fusion, bf16[6144,576]{0,1:T(8,128)(2,1)S(1)} %copy-done.2), kind=kOutput, calls=%fused_computation.31 | convolution fusion | flops 14495514624 | bytes 36962304 | tf_op jit(solution)/shard_map/dot_general | solution.py:35
  167.4 0.0 all-reduce.4.cloned.1.call-update
  167.5 0.0 all-reduce.6.cloned.1.call-start
  167.5 0.0 copy-done
  167.5 20.8 %fusion.13 = f32[6144,576]{0,1:T(8,128)} fusion(bf16[2048,6144]{1,0:T(8,128)(2,1)} %multiply_convert_fusion, bf16[2048,576]{0,1:T(8,128)(2,1)S(1)} %copy-done, f32[576]{0:T(1024)S(1)} %broadcast_add_fusion, f32[2048]{0:T(1024)S(1)} %add_rsqrt_fusion), kind=kOutput, calls=%fused_computation.21 | convolution fusion | flops 14500233216 | bytes 41691392 | tf_op jit(solution)/shard_map/dot_general | solution.py:36
  188.3 0.0 all-reduce.6.cloned.1.call-update
  188.4 61.8 %all-reduce.4.cloned.1.call-done = f32[2048,576]{0,1:T(8,128)} async-done(((f32[2048,576]{0,1:T(8,128)}), f32[2048,576]{0,1:T(8,128)}) %all-reduce.4.cloned.1.call-update) | async-done | bytes 4718608 | tf_op jit(solution)/shard_map/psum | solution.py:35
  250.1 3.5 fusion.11
  253.7 13.1 %all-reduce = (f32[]{:T(128)}, f32[576]{0:T(1024)}) all-reduce(f32[]{:T(128)} %get-tuple-element.10, f32[576]{0:T(1024)S(1)} %get-tuple-element.7), channel_id=1, replica_groups=mesh['dp'=4,'tp'=8] {'dp'}, use_global_device_ids=true, to_apply=%region_6.0 | all-reduce | flops 577 | bytes 4616 | tf_op jit(solution)/shard_map/psum | solution.py:31
  268.1 4.9 fusion.10
  273.0 455.7 %all-reduce.6.cloned.1.call-done = f32[6144,576]{0,1:T(8,128)} async-done(((f32[6144,576]{0,1:T(8,128)}), f32[6144,576]{0,1:T(8,128)}) %all-reduce.6.cloned.1.call-update) | async-done | bytes 14155792 | tf_op jit(solution)/shard_map/psum | solution.py:36
  728.7 12.0 %copy.11 = f32[6144,576]{0,1:T(8,128)} copy(f32[6144,576]{0,1:T(8,128)} %all-reduce.6.cloned.1.call-done) | data formatting | bytes 28311552
  (4 shorter events, 0.1 us)
Async XLA Ops:
  7.2 243.0 %all-reduce.4.cloned.1.call-start = ((), (), s32[]{:S(2)}) async-start(), calls=%async_computation | async-start | bytes 9437184 | tf_op jit(solution)/shard_map/psum | solution.py:35
  10.1 81.7 %copy-start.1 = (f32[2048]{0:T(1024)S(1)}, f32[2048]{0:T(1024)}, u32[]{:S(2)}) copy-start(f32[2048]{0:T(1024)} %param.9) | copy-start | bytes 24580
  105.8 42.2 %copy-start.2 = (bf16[6144,576]{0,1:T(8,128)(2,1)S(1)}, bf16[6144,576]{0,1:T(8,128)(2,1)}, u32[]{:S(2)}) copy-start(bf16[6144,576]{0,1:T(8,128)(2,1)} %param.7) | copy-start | bytes 21233668
  148.0 19.5 %copy-start = (bf16[2048,576]{0,1:T(8,128)(2,1)S(1)}, bf16[2048,576]{0,1:T(8,128)(2,1)}, u32[]{:S(2)}) copy-start(bf16[2048,576]{0,1:T(8,128)(2,1)} %param.5) | copy-start | bytes 7077892
  167.5 561.2 %all-reduce.6.cloned.1.call-start = ((), (), s32[]{:S(2)}) async-start(), calls=%async_computation.1 | async-start | bytes 28311552 | tf_op jit(solution)/shard_map/psum | solution.py:36
Sparse Core Ops, SparseCore 0:
  167.6 82.5 all-reduce.3
  253.2 475.4 all-reduce.5
where the time goes:
time: 749 us
  waiting for transfers between devices  517 us (69%)
  matrix products  96.3 us (13%)
  other arithmetic  54.7 us (7%)
  blocking collectives  51.4 us (7%)
  between operations  16.6 us (2%)
  local copies, waits for them, and re-layouts  12 us (2%)
    psum x1, waiting for transfers between devices, local_step(): lax.psum(lax.dot_general(grad_z, x_rows, (((0,), (0,)), ((), ())), prefer...  456 us
    psum x1, waiting for transfers between devices, local_step(): lax.psum(jnp.dot(grad_z, tab_rows, preferred_element_type=jnp.float32), '...  61.8 us
    dot_general x1, matrix products, local_step(): lax.dot_general(x_rows, tab_rows, (((1,), (1,)), ((), ())), preferred_ele...  56.1 us
    convert_element_type x1, other arithmetic, local_step(): ((stu_exp / stu_sum - tea_exp / tea_sum) * weight * (1.0 - cap_ratio * ca...  42.1 us
    psum x1, blocking collectives, local_step(): tok_stats = lax.psum(part_stats, 'tp')  25.6 us
    dot_general x1, matrix products, local_step(): lax.dot_general(grad_z, x_rows, (((0,), (0,)), ((), ())), preferred_eleme...  20.8 us
    dot_general x1, matrix products, local_step(): jnp.dot(grad_z, tab_rows, preferred_element_type=jnp.float32)  19.4 us
  transfers between devices with their start and end apart: 2, of which 2 were waited for; matrix products, arithmetic and copies ran while one was open for 4% of the time, Pallas kernels for 0%

commit v1 on v0

v1 whole, which is shorter than its diff:
```python
import functools
import jax, jax.numpy as jnp
from jax import lax
from jax.experimental import pallas as pl
from jax.experimental.pallas import tpu as pltpu

from jax.sharding import PartitionSpec as P

MESH = pl.DeviceIdType.MESH
SOFT_CAP = 30.0
CAP_INV = 1.0 / 30.0
CAP_LOG2E = 30.0 * 1.4426950408889634
NORM_EPS = 1e-6
D = 576

def stats_kernel(vt, rs, hid_ref, w_ref, tab_ref, tea_ref, x_ref, xt_ref, st_ref, acc):
    hid = hid_ref[...].astype(jnp.float32)
    inv = lax.rsqrt(jnp.sum(hid * hid, axis=0, keepdims=True) * (1.0 / D) + NORM_EPS)
    xt = hid * inv * (1.0 + w_ref[...])
    xt_ref[...] = xt.astype(jnp.bfloat16)
    x_ref[...] = jnp.transpose(xt).astype(jnp.bfloat16)
    acc[...] = jnp.zeros_like(acc)
    nv = tab_ref.shape[1] // vt
    tb = x_ref.shape[0]

    def step(j, carry):
        cols = pl.ds(pl.multiple_of(j * vt, vt), vt)
        tab = tab_ref[:, cols]
        for i in range(tb // rs):
            rows = pl.ds(i * rs, rs)
            z = jnp.dot(x_ref[rows, :], tab, preferred_element_type=jnp.float32)
            ths = jnp.tanh(z * CAP_INV)
            es = jnp.exp2(ths * CAP_LOG2E)
            tht = jnp.tanh(tea_ref[rows, cols].astype(jnp.float32) * CAP_INV)
            et = jnp.exp2(tht * CAP_LOG2E)
            wt = et * (tht - ths)
            def fold(a):
                r = a[:, 0:128]
                for k in range(1, vt // 128):
                    r = r + a[:, k * 128:(k + 1) * 128]
                return r
            acc[0, rows, :] += fold(es)
            acc[1, rows, :] += fold(et)
            acc[2, rows, :] += fold(wt)
        return carry
    lax.fori_loop(0, nv, step, 0)
    for k in range(3):
        sums = jnp.sum(jnp.transpose(acc[k]), axis=0, keepdims=True)
        for q in range(tb // 128):
            st_ref[pl.ds((k * pl.num_programs(0) + pl.program_id(0)) * (tb // 128) + q, 1), :] = sums[:, q * 128:(q + 1) * 128]


def forward(hid_t, w_col, tab_t, tea, tb=256, vt=2048, rs=128):
    t, v = tea.shape
    return pl.pallas_call(
        functools.partial(stats_kernel, vt, rs),
        grid=(t // tb,),
        out_shape=(jax.ShapeDtypeStruct((t, D), jnp.bfloat16), jax.ShapeDtypeStruct((D, t), jnp.bfloat16), jax.ShapeDtypeStruct((3 * t // 128, 128), jnp.float32)),
        in_specs=[pl.BlockSpec((D, tb), lambda i: (0, i)), pl.BlockSpec((D, 1), lambda i: (0, 0)), pl.BlockSpec((D, v), lambda i: (0, 0), pipeline_mode=pl.Buffered(1)), pl.BlockSpec((tb, v), lambda i: (i, 0))],
        out_specs=(pl.BlockSpec((tb, D), lambda i: (i, 0)), pl.BlockSpec((D, tb), lambda i: (0, i)), pl.BlockSpec((3 * t // 128, 128), lambda i: (0, 0))),
        scratch_shapes=[pltpu.VMEM((3, tb, 128), jnp.float32)],
        compiler_params=pltpu.CompilerParams(vmem_limit_bytes=48 * 1024 * 1024),
        name='forward',
    )(hid_t, w_col, tab_t, tea)


VBLK = 256
TBLK = 256
NPART = 3
PROWS = D // NPART


def backward_kernel(nblk, ntok, tp, dp, x_ref, xt_ref, st_ref, mask_ref, w_ref, hid_ref, tab_ref, tea_ref,
                    out_ref, dh_ref, small_ref, land_ref, gath_ref,
                    part, near, far, dxt, gbuf, tea_buf, tab_buf, coef_s, coef_t, sbuf, mbuf, slab, load, stage, hbuf, acc_a, acc_b, mloc,
                    blk_sem, send1, recv1, send2, recv2, send3, recv3, store_sem, ssem, srecv, msem, mrecv, rsem, rrecv, gsem, grecv,
                    asem, arecv, bsem, brecv, lsem, hsem, osem):
    z = lax.axis_index('dp')
    t = lax.axis_index('tp')
    inner = jnp.logical_or(z == 1, z == 2)
    outer = jnp.logical_or(z == 0, z == 3)
    across = 3 - z
    beside = jnp.where(z < 2, 1 - z, 5 - z)
    nch = nblk * NPART
    ntile = ntok // TBLK
    rows16 = ntok // 128
    slice_cols = ntok // tp

    def remote(src, dst, ssem_, rsem_, **where):
        return pltpu.make_async_remote_copy(src_ref=src, dst_ref=dst, send_sem=ssem_, recv_sem=rsem_, device_id=where, device_id_type=MESH)

    def tea_load(b):
        return pltpu.make_async_copy(tea_ref.at[:, pl.ds(pl.multiple_of(b * VBLK, VBLK), VBLK)], tea_buf.at[b % 2], blk_sem.at[0, b % 2])

    def tab_load(b):
        return pltpu.make_async_copy(tab_ref.at[:, pl.ds(pl.multiple_of(b * VBLK, VBLK), VBLK)], tab_buf.at[b % 2], blk_sem.at[1, b % 2])

    tea_load(0).start()
    tab_load(0).start()
    hid_load = pltpu.make_async_copy(hid_ref.at[:, pl.ds(pl.multiple_of(t * slice_cols, slice_cols), slice_cols)], hbuf, hsem)
    hid_load.start()
    mloc[...] = mask_ref[0:8, :] + mask_ref[8:16, :]

    barrier = pltpu.get_barrier_semaphore()
    for i in range(1, tp):
        pl.semaphore_signal(barrier, inc=1, device_id={'tp': lax.rem(t + i, tp)}, device_id_type=MESH)
    for i in range(1, dp):
        pl.semaphore_signal(barrier, inc=1, device_id={'dp': lax.rem(z + i, dp)}, device_id_type=MESH)
    pl.semaphore_wait(barrier, tp + dp - 2)

    for i in range(1, tp):
        remote(st_ref, sbuf.at[t], ssem.at[i], srecv.at[t], tp=lax.rem(t + i, tp)).start()
    for i in range(1, dp):
        remote(mloc, mbuf.at[z], msem.at[i], mrecv.at[z], dp=lax.rem(z + i, dp)).start()
    sbuf[t] = st_ref[...]
    mbuf[z] = mloc[...]
    for i in range(1, tp):
        j = lax.rem(t + i, tp)
        remote(st_ref, sbuf.at[j], ssem.at[i], srecv.at[j], tp=j).wait_recv()
    for i in range(1, dp):
        j = lax.rem(z + i, dp)
        remote(mloc, mbuf.at[j], msem.at[i], mrecv.at[j], dp=j).wait_recv()
    sums = sbuf[0]
    for i in range(1, tp):
        sums = sums + sbuf[i]
    count = mbuf[0]
    for i in range(1, dp):
        count = count + mbuf[i]
    mask_sum = jnp.sum(jnp.sum(count, axis=0, keepdims=True), axis=1, keepdims=True)
    stu_sum, tea_sum, cross = sums[0:rows16], sums[rows16:2 * rows16], sums[2 * rows16:3 * rows16]
    mask = mask_ref[...]
    kl = SOFT_CAP * cross / tea_sum + jnp.log(stu_sum) - jnp.log(tea_sum)
    lrow = jnp.sum(mask * kl, axis=0, keepdims=True)
    weight = mask / mask_sum
    for coef, norm in ((coef_s, stu_sum), (coef_t, tea_sum)):
        ratio = weight / norm
        for r in range(rows16):
            coef[r * 128:(r + 1) * 128, :] = jnp.transpose(jnp.broadcast_to(ratio[r:r + 1, :], (128, 128)))
    dxt[...] = jnp.zeros_like(dxt)

    def compute(b):
        slot = b % 2
        tea_load(b).wait()
        tab_load(b).wait()

        @pl.when(b + 1 < nblk)
        def _():
            tea_load(b + 1).start()
            tab_load(b + 1).start()

        def tile(i, carry):
            rows = pl.ds(pl.multiple_of(i * TBLK, TBLK), TBLK)
            tab = tab_buf[slot]
            logits = jnp.dot(x_ref[rows, :], tab, preferred_element_type=jnp.float32)
            ths = jnp.tanh(logits * CAP_INV)
            tht = jnp.tanh(tea_buf[slot, rows, :].astype(jnp.float32) * CAP_INV)
            cs, ct = coef_s[rows, :], coef_t[rows, :]
            cs2 = jnp.concatenate([cs, cs], axis=1)
            ct2 = jnp.concatenate([ct, ct], axis=1)
            g = (jnp.exp2(ths * CAP_LOG2E) * cs2 - jnp.exp2(tht * CAP_LOG2E) * ct2) * (1.0 - ths * ths)
            g = g.astype(jnp.bfloat16)
            gbuf[rows, :] = g
            dxt[:, rows] += lax.dot_general(tab, g, (((1,), (1,)), ((), ())), preferred_element_type=jnp.float32)
            return carry
        lax.fori_loop(0, ntile, tile, 0)
        part[pl.ds(b * NPART, NPART)] = jnp.dot(xt_ref[...], gbuf[...], preferred_element_type=jnp.float32).reshape(NPART, PROWS, VBLK)

        @pl.when(outer)
        def _():
            for q in range(NPART):
                c = b * NPART + q
                remote(part.at[c], near.at[c], send1, recv1.at[c], dp=beside).start()

    def place(c):
        return out_ref.at[pl.ds(pl.multiple_of((c % NPART) * PROWS, PROWS), PROWS), pl.ds(pl.multiple_of((c // NPART) * VBLK, VBLK), VBLK)]

    def swap(c):
        return remote(part.at[c], far.at[c], send2, recv2.at[c], dp=across)

    def first(c):
        remote(part.at[c], near.at[c], send1, recv1.at[c], dp=beside).wait_recv()
        part[c] = part[c] + near[c]
        swap(c).start()

    def finish(c):
        swap(c).wait_recv()
        far[c] = far[c] + part[c]
        remote(far.at[c], place(c), send3, recv3, dp=beside).start()
        pltpu.make_async_copy(far.at[c], place(c), store_sem).start()

    def comm(k):
        @pl.when(inner)
        def _():
            first(k)

            @pl.when(k > 0)
            def _():
                finish(k - 1)

    def loop(lo, hi, body):
        def step(k, carry):
            body(k)
            return carry
        lax.fori_loop(lo, hi, step, 0)

    compute(0)

    def both(k):
        compute(k + 1)
        comm(k)
    loop(0, nblk - 1, both)

    def cols_of(j):
        return pl.ds(pl.multiple_of(j * slice_cols, slice_cols), slice_cols)
    for i in range(1, tp):
        j = lax.rem(t + i, tp)
        remote(dxt.at[:, cols_of(j)], land_ref.at[t], rsem.at[i], rrecv.at[t], tp=j).start()
    k1 = nblk - 1
    k2 = k1 + 14
    loop(k1, k2, comm)
    stage[...] = dxt[:, cols_of(t)]

    def gather(k):
        i = k - k2 + 1
        j = lax.rem(t + i, tp)
        remote(dxt.at[:, cols_of(j)], land_ref.at[j], rsem.at[i], rrecv.at[j], tp=j).wait_recv()
        copy = pltpu.make_async_copy(land_ref.at[j], load, lsem)
        copy.start()
        comm(k)
        copy.wait()
        stage[...] += load[...]
    loop(k2, k2 + tp - 1, gather)
    k3 = k2 + tp - 1
    hid_load.wait()
    hid = hbuf[...].astype(jnp.float32)
    inv = lax.rsqrt(jnp.sum(hid * hid, axis=0, keepdims=True) * (1.0 / D) + NORM_EPS)
    normed = hid * inv
    dx = stage[...]
    gain = dx * normed
    gain = sum((gain[:, q * 128:(q + 1) * 128] for q in range(1, slice_cols // 128)), gain[:, 0:128])
    load[...] = jnp.zeros_like(load)
    load[0:D, 0:128] = gain
    slab[...] = jnp.zeros_like(slab)
    for q in range(5):
        lo, hi = q * 128, min(D, q * 128 + 128)
        sq = load[lo:hi, 0:128]
        if hi - lo < 128:
            sq = jnp.concatenate([sq, jnp.zeros((128 - (hi - lo), 128), jnp.float32)], axis=0)
        slab[0:1, lo:lo + 128] = jnp.sum(jnp.transpose(sq), axis=0, keepdims=True)
    slab[1:2, 0:128] = lrow
    grad_n = dx * (1.0 + w_ref[...])
    stage[...] = inv * (grad_n - normed * (jnp.sum(grad_n * normed, axis=0, keepdims=True) * (1.0 / D)))
    for i in range(1, tp):
        j = lax.rem(t + i, tp)
        remote(slab, acc_a.at[t], asem.at[i], arecv.at[t], tp=j).start()
        remote(stage, gath_ref.at[t], gsem.at[i], grecv.at[t], tp=j).start()
    acc_a[t] = slab[...]

    def emit(j):
        hbuf[...] = load[...].astype(jnp.bfloat16)
        copy = pltpu.make_async_copy(hbuf, dh_ref.at[:, cols_of(j)], hsem)
        copy.start()
        copy.wait()
    load[...] = stage[...]
    emit(t)
    k4 = k3 + 14
    loop(k3, k4, comm)
    for i in range(1, tp):
        j = lax.rem(t + i, tp)
        remote(slab, acc_a.at[j], asem.at[i], arecv.at[j], tp=j).wait_recv()
    tot = acc_a[0]
    for i in range(1, tp):
        tot = tot + acc_a[i]
    hbuf_row = lax.broadcasted_iota(jnp.int32, tot.shape, 0) == 0
    acc_b[z] = jnp.where(hbuf_row, tot, slab[...])
    for i in range(1, dp):
        j = lax.rem(z + i, dp)
        remote(acc_b.at[z], acc_b.at[z], bsem.at[i], brecv.at[z], dp=j).start()

    def spread(k):
        i = k - k4 + 1
        j = lax.rem(t + i, tp)
        remote(stage, gath_ref.at[j], gsem.at[i], grecv.at[j], tp=j).wait_recv()
        copy = pltpu.make_async_copy(gath_ref.at[j], load, lsem)
        copy.start()
        comm(k)
        copy.wait()
        emit(j)
    loop(k4, k4 + tp - 1, spread)
    loop(k4 + tp - 1, nch, comm)

    for i in range(1, dp):
        j = lax.rem(z + i, dp)
        remote(acc_b.at[j], acc_b.at[j], bsem.at[i], brecv.at[j], dp=j).wait_recv()
    tot = acc_b[0]
    for i in range(1, dp):
        tot = tot + acc_b[i]
    loss = jnp.sum(tot[1:2, 0:128], axis=1, keepdims=True) / mask_sum
    row = lax.broadcasted_iota(jnp.int32, tot.shape, 0)
    small_ref[...] = jnp.where(row == 1, loss, tot)

    @pl.when(inner)
    def _():
        finish(nch - 1)
        remote(part, far, send2, recv2.at[0], dp=across).wait_send()
        remote(far, far, send3, recv3, dp=beside).wait_send()
        pltpu.make_async_copy(out_ref, out_ref, store_sem).wait()

    @pl.when(outer)
    def _():
        remote(part, near, send1, recv1.at[0], dp=beside).wait_send()
        remote(out_ref, out_ref, send3, recv3, dp=beside).wait_recv()

    for i in range(1, tp):
        j = lax.rem(t + i, tp)
        remote(st_ref, sbuf.at[t], ssem.at[i], srecv.at[t], tp=j).wait_send()
        remote(dxt.at[:, cols_of(j)], land_ref.at[t], rsem.at[i], rrecv.at[t], tp=j).wait_send()
        remote(slab, acc_a.at[t], asem.at[i], arecv.at[t], tp=j).wait_send()
        remote(stage, gath_ref.at[t], gsem.at[i], grecv.at[t], tp=j).wait_send()
    for i in range(1, dp):
        j = lax.rem(z + i, dp)
        remote(mloc, mbuf.at[z], msem.at[i], mrecv.at[z], dp=j).wait_send()
        remote(acc_b.at[z], acc_b.at[z], bsem.at[i], brecv.at[z], dp=j).wait_send()


def backward(mesh, x, xt, stats, mask, w_col, hid_t, tab_t, tea):
    tp, dp = mesh.shape['tp'], mesh.shape['dp']
    ntok, vocab = tea.shape
    nblk = vocab // VBLK
    nch = nblk * NPART
    sl = ntok // tp
    f32, bf16 = jnp.float32, jnp.bfloat16
    dma = pltpu.SemaphoreType.DMA
    vmem = pl.BlockSpec(memory_space=pltpu.VMEM)
    hbm = pl.BlockSpec(memory_space=pl.ANY)
    chunks = pltpu.VMEM((nch, PROWS, VBLK), f32)
    out, dh, small, _, _ = pl.pallas_call(
        functools.partial(backward_kernel, nblk, ntok, tp, dp),
        out_shape=(jax.ShapeDtypeStruct((D, vocab), f32), jax.ShapeDtypeStruct((D, ntok), bf16), jax.ShapeDtypeStruct((8, 640), f32),
                   jax.ShapeDtypeStruct((tp, D, sl), f32), jax.ShapeDtypeStruct((tp, D, sl), f32)),
        in_specs=[vmem, vmem, vmem, vmem, vmem, hbm, hbm, hbm],
        out_specs=(hbm, hbm, vmem, hbm, hbm),
        scratch_shapes=[
            chunks, chunks, chunks, pltpu.VMEM((D, ntok), f32), pltpu.VMEM((ntok, VBLK), bf16), pltpu.VMEM((2, ntok, VBLK), bf16),
            pltpu.VMEM((2, D, VBLK), bf16), pltpu.VMEM((ntok, 128), f32), pltpu.VMEM((ntok, 128), f32), pltpu.VMEM((tp, 3 * ntok // 128, 128), f32),
            pltpu.VMEM((dp, 8, 128), f32), pltpu.VMEM((8, 640), f32), pltpu.VMEM((D, sl), f32), pltpu.VMEM((D, sl), f32), pltpu.VMEM((D, sl), bf16),
            pltpu.VMEM((tp, 8, 640), f32), pltpu.VMEM((dp, 8, 640), f32), pltpu.VMEM((8, 128), f32),
            dma((2, 2)), dma, dma((nch,)), dma, dma((nch,)), dma, dma, dma, dma((tp,)), dma((tp,)), dma((dp,)), dma((dp,)),
            dma((tp,)), dma((tp,)), dma((tp,)), dma((tp,)), dma((tp,)), dma((tp,)), dma((dp,)), dma((dp,)), dma, dma, dma],
        compiler_params=pltpu.CompilerParams(collective_id=0, has_side_effects=True, vmem_limit_bytes=67043328),
        name='backward',
    )(x, xt, stats, mask, w_col, hid_t, tab_t, tea)
    return out, dh, small


def solution(mesh):
    def local_step(hid_rows, w_final, tab_rows, tea_rows, mask_rows):
        w_col = w_final[:, None]
        hid_t, tab_t = hid_rows.T, tab_rows.T
        x, xt, stats = forward(hid_t, w_col, tab_t, tea_rows)
        mask = mask_rows.reshape(-1, 128)
        grad_table, grad_hid, small = backward(mesh, x, xt, stats, mask, w_col, hid_t, tab_t, tea_rows)
        return small[1, 0], grad_hid.T, small[0, :D], grad_table.T

    return jax.shard_map(local_step, mesh=mesh, in_specs=(P('dp', None), P(None), P('tp', None), P('dp', 'tp'), P('dp')), out_specs=(P(), P('dp', None), P(None), P('tp', None)), check_vma=False)
```

time: 749 us -> 438 us (0.58)
  waiting for transfers between devices: 517 us -> 0 us
  Pallas kernels: 0 us -> 414 us
  matrix products: 96.3 us -> 0 us
  other arithmetic: 54.7 us -> 0 us
  blocking collectives: 51.4 us -> 0 us
  between operations: 16.6 us -> 0.66 us
  local copies, waits for them, and re-layouts: 12 us -> 22.4 us
    psum x2 -> x0, waiting for transfers between devices: 517 us -> none  [the longest x1 456 us: local_step(): lax.psum(lax.dot_general(grad_z, x_rows, (((0,), (0,)), ((), ())), prefer...]
    pallas_call x0 -> x2, Pallas kernels: none -> 414 us  [the longest x1 371 us: backward(): pl.pallas_call(functools.partial(backward_kernel, nblk, ntok, tp, dp), ou...]
    dot_general x3 -> x0, matrix products: 96.3 us -> none  [the longest x1 56.1 us: local_step(): lax.dot_general(x_rows, tab_rows, (((1,), (1,)), ((), ())), preferred_ele...]
    psum x3 -> x0, blocking collectives: 51.4 us -> none  [the longest x1 25.6 us: local_step(): tok_stats = lax.psum(part_stats, 'tp')]
    convert_element_type x2 -> x0, other arithmetic: 47 us -> none  [the longest x1 42.1 us: local_step(): ((stu_exp / stu_sum - tea_exp / tea_sum) * weight * (1.0 - cap_ratio * ca...]
    unnamed x7 -> x10, local copies, waits for them, and re-layouts: 12 us -> 19 us
  transfers between devices with their start and end apart: 2 -> 0, of which waited for: 2 -> 0; matrix products, arithmetic and copies ran while one was open for 4% -> 0% of each run, Pallas kernels for 0% -> 0%
where the time goes in v1:
time: 438 us; the launch traced here: 437 us
  Pallas kernels  414 us (95%)
  local copies, waits for them, and re-layouts  22.4 us (5%)
    pallas_call x1, Pallas kernels, backward(): pl.pallas_call(functools.partial(backward_kernel, nblk, ntok, tp, dp), ou...  371 us
    pallas_call x1, Pallas kernels, forward(): pl.pallas_call(functools.partial(stats_kernel, vt, rs), grid=(t // tb,),...  42.9 us
    unnamed x10, local copies, waits for them, and re-layouts  19 us

profile of v1, /device:TPU:0, one launch (start us, length us, event | category | flops | bytes accessed | tf_op | source)
XLA Modules:
  0.0 437.3 jit_solution(12459049213755491247)
XLA Ops:
  0.6 0.8 broadcast_in_dim.4.w_ref
  1.5 0.0 copy-start
  1.5 1.7 copy-done
  3.1 0.0 copy-start.1
  3.1 42.9 %forward.1 = (bf16[2048,576]{1,0:T(8,128)(2,1)}, bf16[576,2048]{1,0:T(8,128)(2,1)S(1)}, f32[48,128]{1,0:T(8,128)S(1)}) custom-call(bf16[576,2048]{1,0:T(8,128)(2,1)S(1)} %bitcast.7, f32[576,1]{1,0:T(8,128)S(1)} %broadcast_in_dim.4.w_ref, bf16[576,6144]{1,0:T(8,128)(2,1)} %bitcast.8, bf16[2048,6144]{1,0:T(8,128)(2,1)} %tea_ref.3), custom_call_target="tpu_custom_call" | custom-call | tf_op jit(solution)/shard_map/forward/pallas_call | solution.py:55
  46.1 0.0 copy-done.1
  46.1 0.0 copy-start.2
  46.1 1.4 copy-done.2
  47.5 0.0 copy-start.3
  47.5 0.6 copy-done.3
  48.1 371.4 %backward.1 = (f32[576,6144]{1,0:T(8,128)}, bf16[576,2048]{1,0:T(8,128)(2,1)}, f32[8,640]{1,0:T(8,128)}, f32[8,576,256]{2,1,0:T(8,128)}, f32[8,576,256]{2,1,0:T(8,128)}) custom-call(bf16[2048,576]{1,0:T(8,128)(2,1)} %get-tuple-element.10.x_ref, bf16[576,2048]{1,0:T(8,128)(2,1)} %copy-done.2, f32[48,128]{1,0:T(8,128)} %copy-done.3, f32[16,128]{1,0:T(8,128)} %bitcast.12, ...), custom_call_target="tpu_custom_call" | custom-call | tf_op jit(solution)/shard_map/backward/pallas_call | solution.py:337
  419.4 1.2 slice.6
  420.6 1.3 slice_reduce_fusion
  421.9 3.4 copy.13
  425.3 12.0 %copy.14 = f32[6144,576]{0,1:T(8,128)} copy(f32[6144,576]{0,1:T(8,128)} %bitcast.10) | data formatting | bytes 28311552
Async XLA Ops:
  1.5 1.7 copy-start
  3.1 42.9 %copy-start.1 = (f32[576,1]{1,0:T(8,128)}, f32[576,1]{1,0:T(8,128)S(1)}, u32[]{:S(2)}) copy-start(f32[576,1]{1,0:T(8,128)S(1)} %broadcast_in_dim.4.w_ref) | copy-start | bytes 6916
  46.1 1.4 copy-start.2
  47.5 0.6 copy-start.3

commit v2 on v1

--- a/solution.py
+++ b/solution.py
@@ -50,7 +50,7 @@
             st_ref[pl.ds((k * pl.num_programs(0) + pl.program_id(0)) * (tb // 128) + q, 1), :] = sums[:, q * 128:(q + 1) * 128]
 
 
-def forward(hid_t, w_col, tab_t, tea, tb=256, vt=2048, rs=128):
+def forward(hid_t, w_col, tab_t, tea, tb=512, vt=2048, rs=128):
     t, v = tea.shape
     return pl.pallas_call(
         functools.partial(stats_kernel, vt, rs),
@@ -59,22 +59,23 @@
         in_specs=[pl.BlockSpec((D, tb), lambda i: (0, i)), pl.BlockSpec((D, 1), lambda i: (0, 0)), pl.BlockSpec((D, v), lambda i: (0, 0), pipeline_mode=pl.Buffered(1)), pl.BlockSpec((tb, v), lambda i: (i, 0))],
         out_specs=(pl.BlockSpec((tb, D), lambda i: (i, 0)), pl.BlockSpec((D, tb), lambda i: (0, i)), pl.BlockSpec((3 * t // 128, 128), lambda i: (0, 0))),
         scratch_shapes=[pltpu.VMEM((3, tb, 128), jnp.float32)],
-        compiler_params=pltpu.CompilerParams(vmem_limit_bytes=48 * 1024 * 1024),
+        compiler_params=pltpu.CompilerParams(vmem_limit_bytes=67043328),
         name='forward',
     )(hid_t, w_col, tab_t, tea)
 
 
 VBLK = 256
-TBLK = 256
+TBLK = 1024
+LAG = 2
 NPART = 3
 PROWS = D // NPART
 
 
-def backward_kernel(nblk, ntok, tp, dp, x_ref, xt_ref, st_ref, mask_ref, w_ref, hid_ref, tab_ref, tea_ref,
+def backward_kernel(nblk, ntok, tp, dp, x_hbm, xt_hbm, st_ref, mask_ref, w_ref, hid_ref, tab_ref, tea_ref,
                     out_ref, dh_ref, small_ref, land_ref, gath_ref,
-                    part, near, far, dxt, gbuf, tea_buf, tab_buf, coef_s, coef_t, sbuf, mbuf, slab, load, stage, hbuf, acc_a, acc_b, mloc,
+                    x_ref, xt_ref, part, near, far, dxt, gbuf, tea_buf, tab_buf, coef_s, coef_t, sbuf, mbuf, slab, load, stage, hbuf, acc_a, acc_b, mloc,
                     blk_sem, send1, recv1, send2, recv2, send3, recv3, store_sem, ssem, srecv, msem, mrecv, rsem, rrecv, gsem, grecv,
-                    asem, arecv, bsem, brecv, lsem, hsem, osem):
+                    asem, arecv, bsem, brecv, lsem, hsem, osem, xsem):
     z = lax.axis_index('dp')
     t = lax.axis_index('tp')
     inner = jnp.logical_or(z == 1, z == 2)
@@ -82,7 +83,6 @@
     across = 3 - z
     beside = jnp.where(z < 2, 1 - z, 5 - z)
     nch = nblk * NPART
-    ntile = ntok // TBLK
     rows16 = ntok // 128
     slice_cols = ntok // tp
 
@@ -95,9 +95,13 @@
     def tab_load(b):
         return pltpu.make_async_copy(tab_ref.at[:, pl.ds(pl.multiple_of(b * VBLK, VBLK), VBLK)], tab_buf.at[b % 2], blk_sem.at[1, b % 2])
 
+    x_load = pltpu.make_async_copy(x_hbm, x_ref, xsem.at[0])
+    xt_load = pltpu.make_async_copy(xt_hbm, xt_ref, xsem.at[1])
+    tab_load(0).start()
+    x_load.start()
     tea_load(0).start()
-    tab_load(0).start()
-    hid_load = pltpu.make_async_copy(hid_ref.at[:, pl.ds(pl.multiple_of(t * slice_cols, slice_cols), slice_cols)], hbuf, hsem)
+    xt_load.start()
+    hid_load = pltpu.make_async_copy(hid_ref.at[:, pl.ds(pl.multiple_of(t * slice_cols, slice_cols), slice_cols)], hbuf.at[0], hsem)
     hid_load.start()
     mloc[...] = mask_ref[0:8, :] + mask_ref[8:16, :]
 
@@ -138,8 +142,7 @@
             coef[r * 128:(r + 1) * 128, :] = jnp.transpose(jnp.broadcast_to(ratio[r:r + 1, :], (128, 128)))
     dxt[...] = jnp.zeros_like(dxt)
 
-    def compute(b):
-        slot = b % 2
+    def fetch(b):
         tea_load(b).wait()
         tab_load(b).wait()
 
@@ -148,21 +151,22 @@
             tea_load(b + 1).start()
             tab_load(b + 1).start()
 
-        def tile(i, carry):
-            rows = pl.ds(pl.multiple_of(i * TBLK, TBLK), TBLK)
-            tab = tab_buf[slot]
-            logits = jnp.dot(x_ref[rows, :], tab, preferred_element_type=jnp.float32)
-            ths = jnp.tanh(logits * CAP_INV)
-            tht = jnp.tanh(tea_buf[slot, rows, :].astype(jnp.float32) * CAP_INV)
-            cs, ct = coef_s[rows, :], coef_t[rows, :]
-            cs2 = jnp.concatenate([cs, cs], axis=1)
-            ct2 = jnp.concatenate([ct, ct], axis=1)
-            g = (jnp.exp2(ths * CAP_LOG2E) * cs2 - jnp.exp2(tht * CAP_LOG2E) * ct2) * (1.0 - ths * ths)
-            g = g.astype(jnp.bfloat16)
-            gbuf[rows, :] = g
-            dxt[:, rows] += lax.dot_general(tab, g, (((1,), (1,)), ((), ())), preferred_element_type=jnp.float32)
-            return carry
-        lax.fori_loop(0, ntile, tile, 0)
+    def tile(b, i):
+        slot = b % 2
+        rows = pl.ds(i * TBLK, TBLK)
+        tab = tab_buf[slot]
+        logits = jnp.dot(x_ref[rows, :], tab, preferred_element_type=jnp.float32)
+        ths = jnp.tanh(logits * CAP_INV)
+        tht = jnp.tanh(tea_buf[slot, rows, :].astype(jnp.float32) * CAP_INV)
+        cs, ct = coef_s[rows, :], coef_t[rows, :]
+        cs2 = jnp.concatenate([cs, cs], axis=1)
+        ct2 = jnp.concatenate([ct, ct], axis=1)
+        g = (jnp.exp2(ths * CAP_LOG2E) * cs2 - jnp.exp2(tht * CAP_LOG2E) * ct2) * (1.0 - ths * ths)
+        g = g.astype(jnp.bfloat16)
+        gbuf[rows, :] = g
+        dxt[:, rows] += lax.dot_general(tab, g, (((1,), (1,)), ((), ())), preferred_element_type=jnp.float32)
+
+    def table(b):
         part[pl.ds(b * NPART, NPART)] = jnp.dot(xt_ref[...], gbuf[...], preferred_element_type=jnp.float32).reshape(NPART, PROWS, VBLK)
 
         @pl.when(outer)
@@ -191,11 +195,13 @@
     def comm(k):
         @pl.when(inner)
         def _():
-            first(k)
-
-            @pl.when(k > 0)
-            def _():
-                finish(k - 1)
+            for q in range(1):
+                c = 1 * k + q
+                first(c)
+
+                @pl.when(c >= LAG)
+                def _():
+                    finish(c - LAG)
 
     def loop(lo, hi, body):
         def step(k, carry):
@@ -203,47 +209,73 @@
             return carry
         lax.fori_loop(lo, hi, step, 0)
 
-    compute(0)
-
-    def both(k):
-        compute(k + 1)
-        comm(k)
-    loop(0, nblk - 1, both)
+    def half(h):
+        b = h // 2
+
+        @pl.when(h % 2 == 0)
+        def _():
+            fetch(b)
+            tile(b, 0)
+
+        @pl.when(h % 2 == 1)
+        def _():
+            tile(b, 1)
+            table(b)
+
+    def both(h):
+        half(h)
+
+        @pl.when(jnp.logical_and(h >= 2, (h - 2) % 4 != 3))
+        def _():
+            comm(h - 2 - (h - 2) // 4)
+    x_load.wait()
+    xt_load.wait()
+    loop(0, 2 * nblk, both)
 
     def cols_of(j):
         return pl.ds(pl.multiple_of(j * slice_cols, slice_cols), slice_cols)
     for i in range(1, tp):
         j = lax.rem(t + i, tp)
         remote(dxt.at[:, cols_of(j)], land_ref.at[t], rsem.at[i], rrecv.at[t], tp=j).start()
-    k1 = nblk - 1
-    k2 = k1 + 14
+    k1 = 2 * nblk - 2 - (2 * nblk - 2) // 4
+    k2 = k1 + 13
     loop(k1, k2, comm)
     stage[...] = dxt[:, cols_of(t)]
 
+    def landed(i):
+        j = lax.rem(t + i, tp)
+        remote(dxt.at[:, cols_of(j)], land_ref.at[j], rsem.at[i], rrecv.at[j], tp=j).wait_recv()
+        return pltpu.make_async_copy(land_ref.at[j], load.at[i % 2], lsem.at[i % 2])
+
     def gather(k):
-        i = k - k2 + 1
-        j = lax.rem(t + i, tp)
-        remote(dxt.at[:, cols_of(j)], land_ref.at[j], rsem.at[i], rrecv.at[j], tp=j).wait_recv()
-        copy = pltpu.make_async_copy(land_ref.at[j], load, lsem)
-        copy.start()
+        i = 2 * (k - k2) + 1
+        one, two = landed(i), landed(i + 1)
+        one.start()
+        two.start()
         comm(k)
-        copy.wait()
-        stage[...] += load[...]
-    loop(k2, k2 + tp - 1, gather)
-    k3 = k2 + tp - 1
+        one.wait()
+        stage[...] += load[1]
+        two.wait()
+        stage[...] += load[0]
+    k3 = k2 + tp // 2
+    loop(k2, k3 - 1, gather)
+    last = landed(tp - 1)
+    last.start()
+    comm(k3 - 1)
+    last.wait()
+    stage[...] += load[1]
     hid_load.wait()
-    hid = hbuf[...].astype(jnp.float32)
+    hid = hbuf[0].astype(jnp.float32)
     inv = lax.rsqrt(jnp.sum(hid * hid, axis=0, keepdims=True) * (1.0 / D) + NORM_EPS)
     normed = hid * inv
     dx = stage[...]
     gain = dx * normed
     gain = sum((gain[:, q * 128:(q + 1) * 128] for q in range(1, slice_cols // 128)), gain[:, 0:128])
-    load[...] = jnp.zeros_like(load)
-    load[0:D, 0:128] = gain
+    load[0, :, 0:128] = gain
     slab[...] = jnp.zeros_like(slab)
     for q in range(5):
         lo, hi = q * 128, min(D, q * 128 + 128)
-        sq = load[lo:hi, 0:128]
+        sq = load[0, lo:hi, 0:128]
         if hi - lo < 128:
             sq = jnp.concatenate([sq, jnp.zeros((128 - (hi - lo), 128), jnp.float32)], axis=0)
         slab[0:1, lo:lo + 128] = jnp.sum(jnp.transpose(sq), axis=0, keepdims=True)
@@ -256,15 +288,15 @@
         remote(stage, gath_ref.at[t], gsem.at[i], grecv.at[t], tp=j).start()
     acc_a[t] = slab[...]
 
-    def emit(j):
-        hbuf[...] = load[...].astype(jnp.bfloat16)
-        copy = pltpu.make_async_copy(hbuf, dh_ref.at[:, cols_of(j)], hsem)
-        copy.start()
-        copy.wait()
-    load[...] = stage[...]
-    emit(t)
-    k4 = k3 + 14
+    def emit(j, src, slot):
+        hbuf[slot] = src.astype(jnp.bfloat16)
+        return pltpu.make_async_copy(hbuf.at[slot], dh_ref.at[:, cols_of(j)], osem.at[slot])
+    own = emit(t, stage[...], 1)
+    own.start()
+    nstep = nch // 1
+    k4 = nstep - tp // 2 - 1
     loop(k3, k4, comm)
+    own.wait()
     for i in range(1, tp):
         j = lax.rem(t + i, tp)
         remote(slab, acc_a.at[j], asem.at[i], arecv.at[j], tp=j).wait_recv()
@@ -277,17 +309,34 @@
         j = lax.rem(z + i, dp)
         remote(acc_b.at[z], acc_b.at[z], bsem.at[i], brecv.at[z], dp=j).start()
 
+    def spread_load(i):
+        j = lax.rem(t + i, tp)
+        remote(stage, gath_ref.at[j], gsem.at[i], grecv.at[j], tp=j).wait_recv()
+        return pltpu.make_async_copy(gath_ref.at[j], load.at[i % 2], lsem.at[i % 2])
+
     def spread(k):
-        i = k - k4 + 1
-        j = lax.rem(t + i, tp)
-        remote(stage, gath_ref.at[j], gsem.at[i], grecv.at[j], tp=j).wait_recv()
-        copy = pltpu.make_async_copy(gath_ref.at[j], load, lsem)
-        copy.start()
+        i = 2 * (k - k4) + 1
+        one, two = spread_load(i), spread_load(i + 1)
+        one.start()
+        two.start()
         comm(k)
-        copy.wait()
-        emit(j)
-    loop(k4, k4 + tp - 1, spread)
-    loop(k4 + tp - 1, nch, comm)
+        one.wait()
+        out1 = emit(lax.rem(t + i, tp), load[1], 1)
+        out1.start()
+        two.wait()
+        out2 = emit(lax.rem(t + i + 1, tp), load[0], 0)
+        out2.start()
+        out1.wait()
+        out2.wait()
+    loop(k4, k4 + tp // 2 - 1, spread)
+    tail = spread_load(tp - 1)
+    tail.start()
+    comm(k4 + tp // 2 - 1)
+    tail.wait()
+    final = emit(lax.rem(t + tp - 1, tp), load[1], 1)
+    final.start()
+    loop(k4 + tp // 2, nstep, comm)
+    final.wait()
 
     for i in range(1, dp):
         j = lax.rem(z + i, dp)
@@ -301,7 +350,8 @@
 
     @pl.when(inner)
     def _():
-        finish(nch - 1)
+        for c in range(nch - LAG, nch):
+            finish(c)
         remote(part, far, send2, recv2.at[0], dp=across).wait_send()
         remote(far, far, send3, recv3, dp=beside).wait_send()
         pltpu.make_async_copy(out_ref, out_ref, store_sem).wait()
@@ -338,19 +388,43 @@
         functools.partial(backward_kernel, nblk, ntok, tp, dp),
         out_shape=(jax.ShapeDtypeStruct((D, vocab), f32), jax.ShapeDtypeStruct((D, ntok), bf16), jax.ShapeDtypeStruct((8, 640), f32),
                    jax.ShapeDtypeStruct((tp, D, sl), f32), jax.ShapeDtypeStruct((tp, D, sl), f32)),
-        in_specs=[vmem, vmem, vmem, vmem, vmem, hbm, hbm, hbm],
+        in_specs=[hbm, hbm, vmem, vmem, vmem, hbm, hbm, hbm],
         out_specs=(hbm, hbm, vmem, hbm, hbm),
         scratch_shapes=[
-            chunks, chunks, chunks, pltpu.VMEM((D, ntok), f32), pltpu.VMEM((ntok, VBLK), bf16), pltpu.VMEM((2, ntok, VBLK), bf16),
+            pltpu.VMEM((ntok, D), bf16), pltpu.VMEM((D, ntok), bf16), chunks, chunks, chunks, pltpu.VMEM((D, ntok), f32), pltpu.VMEM((ntok, VBLK), bf16), pltpu.VMEM((2, ntok, VBLK), bf16),
             pltpu.VMEM((2, D, VBLK), bf16), pltpu.VMEM((ntok, 128), f32), pltpu.VMEM((ntok, 128), f32), pltpu.VMEM((tp, 3 * ntok // 128, 128), f32),
-            pltpu.VMEM((dp, 8, 128), f32), pltpu.VMEM((8, 640), f32), pltpu.VMEM((D, sl), f32), pltpu.VMEM((D, sl), f32), pltpu.VMEM((D, sl), bf16),
+            pltpu.VMEM((dp, 8, 128), f32), pltpu.VMEM((8, 640), f32), pltpu.VMEM((2, D, sl), f32), pltpu.VMEM((D, sl), f32), pltpu.VMEM((2, D, sl), bf16),
             pltpu.VMEM((tp, 8, 640), f32), pltpu.VMEM((dp, 8, 640), f32), pltpu.VMEM((8, 128), f32),
             dma((2, 2)), dma, dma((nch,)), dma, dma((nch,)), dma, dma, dma, dma((tp,)), dma((tp,)), dma((dp,)), dma((dp,)),
-            dma((tp,)), dma((tp,)), dma((tp,)), dma((tp,)), dma((tp,)), dma((tp,)), dma((dp,)), dma((dp,)), dma, dma, dma],
+            dma((tp,)), dma((tp,)), dma((tp,)), dma((tp,)), dma((tp,)), dma((tp,)), dma((dp,)), dma((dp,)), dma((2,)), dma, dma((2,)), dma((2,))],
         compiler_params=pltpu.CompilerParams(collective_id=0, has_side_effects=True, vmem_limit_bytes=67043328),
         name='backward',
     )(x, xt, stats, mask, w_col, hid_t, tab_t, tea)
     return out, dh, small
+
+
+def emit_kernel(table_ref, dh_ref, small_ref, table_out, dh_out, gain_out, loss_out):
+    table_out[...] = table_ref[...]
+    dh_out[...] = dh_ref[...]
+    gain_out[...] = small_ref[0:1, 0:D]
+    loss_out[...] = small_ref[1:2, 0:1]
+
+
+def emit(table, dh, small, rows=48):
+    vocab, ntok = table.shape[1], dh.shape[1]
+    band = pl.BlockSpec((rows, vocab), lambda i: (i, 0))
+    hid = pl.BlockSpec((rows, ntok), lambda i: (i, 0))
+
+    def whole(*shape):
+        return pl.BlockSpec(shape, lambda i: (0, 0))
+    return pl.pallas_call(
+        emit_kernel,
+        grid=(D // rows,),
+        out_shape=(jax.ShapeDtypeStruct(table.shape, table.dtype), jax.ShapeDtypeStruct(dh.shape, dh.dtype), jax.ShapeDtypeStruct((1, D), jnp.float32), jax.ShapeDtypeStruct((1, 1), jnp.float32)),
+        in_specs=[band, hid, whole(*small.shape)],
+        out_specs=(band, hid, whole(1, D), whole(1, 1)),
+        name='emit',
+    )(table, dh, small)
 
 
 def solution(mesh):
@@ -360,6 +434,7 @@
         x, xt, stats = forward(hid_t, w_col, tab_t, tea_rows)
         mask = mask_rows.reshape(-1, 128)
         grad_table, grad_hid, small = backward(mesh, x, xt, stats, mask, w_col, hid_t, tab_t, tea_rows)
-        return small[1, 0], grad_hid.T, small[0, :D], grad_table.T
+        grad_table, grad_hid, gain, loss = emit(grad_table, grad_hid, small)
+        return loss[0, 0], grad_hid.T, gain[0], grad_table.T
 
     return jax.shard_map(local_step, mesh=mesh, in_specs=(P('dp', None), P(None), P('tp', None), P('dp', 'tp'), P('dp')), out_specs=(P(), P('dp', None), P(None), P('tp', None)), check_vma=False)

time: 438 us -> 399 us (0.911)
  local copies, waits for them, and re-layouts: 22.4 us -> 1.57 us
  Pallas kernels: 414 us -> 395 us
    pallas_call x1, Pallas kernels: 371 us -> 339 us  [backward(): pl.pallas_call(functools.partial(backward_kernel, nblk, ntok, tp, dp), ou...]
    unnamed x10 -> x0, local copies, waits for them, and re-layouts: 19 us -> none
    pallas_call x0 -> x1, Pallas kernels: none -> 15.2 us  [emit(): pl.pallas_call(emit_kernel, grid=(D // rows,), out_shape=(jax.ShapeDtypeS...]
where the time goes in v2:
time: 399 us; the launch traced here: 398 us
  Pallas kernels  395 us (99%)
    pallas_call x1, Pallas kernels, backward(): pl.pallas_call(functools.partial(backward_kernel, nblk, ntok, tp, dp), ou...  339 us
    pallas_call x1, Pallas kernels, forward(): pl.pallas_call(functools.partial(stats_kernel, vt, rs), grid=(t // tb,),...  40.2 us
    pallas_call x1, Pallas kernels, emit(): pl.pallas_call(emit_kernel, grid=(D // rows,), out_shape=(jax.ShapeDtypeS...  15.2 us

profile of v2, /device:TPU:0, one launch (start us, length us, event | category | flops | bytes accessed | tf_op | source)
XLA Modules:
  0.0 398.1 jit_solution(9231834038344472093)
XLA Ops:
  0.6 1.6 broadcast_in_dim.4.w_ref
  2.2 40.2 %forward.1 = (bf16[2048,576]{1,0:T(8,128)(2,1)}, bf16[576,2048]{1,0:T(8,128)(2,1)}, f32[48,128]{1,0:T(8,128)}) custom-call(bf16[576,2048]{1,0:T(8,128)(2,1)} %bitcast.8, f32[576,1]{1,0:T(8,128)} %broadcast_in_dim.4.w_ref, bf16[576,6144]{1,0:T(8,128)(2,1)} %bitcast.6, bf16[2048,6144]{1,0:T(8,128)(2,1)} %tea_ref.3), custom_call_target="tpu_custom_call" | custom-call | tf_op jit(solution)/shard_map/forward/pallas_call | solution.py:55
  42.4 339.2 %backward.1 = (f32[576,6144]{1,0:T(8,128)}, bf16[576,2048]{1,0:T(8,128)(2,1)}, f32[8,640]{1,0:T(8,128)}, f32[8,576,256]{2,1,0:T(8,128)}, f32[8,576,256]{2,1,0:T(8,128)}) custom-call(bf16[2048,576]{1,0:T(8,128)(2,1)} %get-tuple-element.14.x_hbm, bf16[576,2048]{1,0:T(8,128)(2,1)} %get-tuple-element.15.xt_hbm, f32[48,128]{1,0:T(8,128)} %get-tuple-element.16.st_ref, ...), custom_call_target="tpu_custom_call" | custom-call | tf_op jit(solution)/shard_map/backward/pallas_call | solution.py:387
  381.6 15.2 %emit.1 = (f32[576,6144]{1,0:T(8,128)}, bf16[576,2048]{1,0:T(8,128)(2,1)}, f32[1,576]{1,0:T(1,128)}, f32[1,1]{1,0:T(1,128)}) custom-call(f32[576,6144]{1,0:T(8,128)} %get-tuple-element.17.table_ref, bf16[576,2048]{1,0:T(8,128)(2,1)} %get-tuple-element.18.dh_ref, f32[8,640]{1,0:T(8,128)} %get-tuple-element.19.small_ref), custom_call_target="tpu_custom_call" | custom-call | tf_op jit(solution)/shard_map/emit/pallas_call | solution.py:420
  396.8 1.3 reduce

commit v3 on v2

--- a/solution.py
+++ b/solution.py
@@ -406,7 +406,7 @@
 def emit_kernel(table_ref, dh_ref, small_ref, table_out, dh_out, gain_out, loss_out):
     table_out[...] = table_ref[...]
     dh_out[...] = dh_ref[...]
-    gain_out[...] = small_ref[0:1, 0:D]
+    gain_out[...] = small_ref[0, 0:D]
     loss_out[...] = small_ref[1:2, 0:1]
 
 
@@ -420,9 +420,9 @@
     return pl.pallas_call(
         emit_kernel,
         grid=(D // rows,),
-        out_shape=(jax.ShapeDtypeStruct(table.shape, table.dtype), jax.ShapeDtypeStruct(dh.shape, dh.dtype), jax.ShapeDtypeStruct((1, D), jnp.float32), jax.ShapeDtypeStruct((1, 1), jnp.float32)),
+        out_shape=(jax.ShapeDtypeStruct(table.shape, table.dtype), jax.ShapeDtypeStruct(dh.shape, dh.dtype), jax.ShapeDtypeStruct((D,), jnp.float32), jax.ShapeDtypeStruct((1, 1), jnp.float32)),
         in_specs=[band, hid, whole(*small.shape)],
-        out_specs=(band, hid, whole(1, D), whole(1, 1)),
+        out_specs=(band, hid, pl.BlockSpec((D,), lambda i: (0,)), whole(1, 1)),
         name='emit',
     )(table, dh, small)
 
@@ -435,6 +435,6 @@
         mask = mask_rows.reshape(-1, 128)
         grad_table, grad_hid, small = backward(mesh, x, xt, stats, mask, w_col, hid_t, tab_t, tea_rows)
         grad_table, grad_hid, gain, loss = emit(grad_table, grad_hid, small)
-        return loss[0, 0], grad_hid.T, gain[0], grad_table.T
+        return loss.reshape(()), grad_hid.T, gain, grad_table.T
 
     return jax.shard_map(local_step, mesh=mesh, in_specs=(P('dp', None), P(None), P('tp', None), P('dp', 'tp'), P('dp')), out_specs=(P(), P('dp', None), P(None), P('tp', None)), check_vma=False)

time: 399 us -> 398 us (level)
  no operation moved by 1% of the time
where the time goes in v3:
time: 398 us; the launch traced here: 397 us
  Pallas kernels  395 us (99%)
    pallas_call x1, Pallas kernels, backward(): pl.pallas_call(functools.partial(backward_kernel, nblk, ntok, tp, dp), ou...  339 us
    pallas_call x1, Pallas kernels, forward(): pl.pallas_call(functools.partial(stats_kernel, vt, rs), grid=(t // tb,),...  40.1 us
    pallas_call x1, Pallas kernels, emit(): pl.pallas_call(emit_kernel, grid=(D // rows,), out_shape=(jax.ShapeDtypeS...  15.2 us

profile of v3, /device:TPU:0, one launch (start us, length us, event | category | flops | bytes accessed | tf_op | source)
XLA Modules:
  0.0 396.8 jit_solution(3860439698524291831)
XLA Ops:
  0.6 1.6 broadcast_in_dim.4.w_ref
  2.2 40.1 %forward.1 = (bf16[2048,576]{1,0:T(8,128)(2,1)}, bf16[576,2048]{1,0:T(8,128)(2,1)}, f32[48,128]{1,0:T(8,128)}) custom-call(bf16[576,2048]{1,0:T(8,128)(2,1)} %bitcast.8, f32[576,1]{1,0:T(8,128)} %broadcast_in_dim.4.w_ref, bf16[576,6144]{1,0:T(8,128)(2,1)} %bitcast.6, bf16[2048,6144]{1,0:T(8,128)(2,1)} %tea_ref.3), custom_call_target="tpu_custom_call" | custom-call | tf_op jit(solution)/shard_map/forward/pallas_call | solution.py:55
  42.3 339.3 %backward.1 = (f32[576,6144]{1,0:T(8,128)}, bf16[576,2048]{1,0:T(8,128)(2,1)}, f32[8,640]{1,0:T(8,128)}, f32[8,576,256]{2,1,0:T(8,128)}, f32[8,576,256]{2,1,0:T(8,128)}) custom-call(bf16[2048,576]{1,0:T(8,128)(2,1)} %get-tuple-element.14.x_hbm, bf16[576,2048]{1,0:T(8,128)(2,1)} %get-tuple-element.15.xt_hbm, f32[48,128]{1,0:T(8,128)} %get-tuple-element.16.st_ref, ...), custom_call_target="tpu_custom_call" | custom-call | tf_op jit(solution)/shard_map/backward/pallas_call | solution.py:387
  381.6 15.2 %emit.1 = (f32[576,6144]{1,0:T(8,128)}, bf16[576,2048]{1,0:T(8,128)(2,1)}, f32[576]{0:T(1024)}, f32[1,1]{1,0:T(1,128)}) custom-call(f32[576,6144]{1,0:T(8,128)} %get-tuple-element.17.table_ref, bf16[576,2048]{1,0:T(8,128)(2,1)} %get-tuple-element.18.dh_ref, f32[8,640]{1,0:T(8,128)} %get-tuple-element.19.small_ref), custom_call_target="tpu_custom_call" | custom-call | tf_op jit(solution)/shard_map/emit/pallas_call | solution.py:420
